TPU v7x, 32 devices: a whole 2x2x4 slice. The times are simulated.
32 devices in a mesh: ctx: 8 (over z, core), tp: 4 (over y, x).
Axes of the slice: x: 2, y: 2, z: 4, core: 2. Of those that a mesh axis runs over, the one named last changes fastest.
Arguments:
- tokens: bfloat16 [2, 4096, 8192], P(None, 'ctx', 'tp'), may hold values from -14 to 14
- norm_gain: float32 [8192], replicated, may hold values from 0.5 to 1.5
- span_order: int32 [2, 16], replicated, may hold values from 0 to 15, each once within a row
- w_query: bfloat16 [8192, 4096], P('ctx', 'tp'), may hold values from -0.10122281 to 0.10122281
- w_key: bfloat16 [8192, 1024], P('ctx', 'tp'), may hold values from -0.10122281 to 0.10122281
- value_weight: bfloat16 [8192, 1024], P('ctx', 'tp'), may hold values from -0.0625 to 0.0625
- w_out: bfloat16 [4096, 8192], P('tp', 'ctx'), may hold values from -0.75 to 0.75
Outputs:
- mixed: bfloat16 [2, 4096, 8192], P(None, 'ctx', 'tp')
Inputs may be any that keep to these rules, and one draw needn't show every extreme that they name: Each row of span_order names every one of the 2 * 8 blocks of positions once; stored block b of a sequence holds positions span_order[b] * 256 onwards, in order.
All inputs are finite; a program needn't handle non-finite values.
Results may differ from a plain program's by a relative error of at most 0.014.
Values may be sent and summed in bfloat16 or wider, within the bound.
A program may use at most 128 MiB of HBM per device.

v0:
```python
import math
import jax
import jax.numpy as jnp
from jax import lax
from jax.sharding import PartitionSpec as P

HEAD_DIM = 128
theta_base = 500000.0
norm_eps = 1e-05
masked_score = -1e30


def normalize(flat_rows, norm_gain):
    wide = flat_rows.astype(jnp.float32)
    factor = lax.rsqrt(jnp.mean(wide * wide, axis=-1, keepdims=True) + norm_eps)
    return (wide * factor * norm_gain).astype(jnp.bfloat16)


def positions_of(span_order, first, count, block_rows):
    stored = first + jnp.arange(count, dtype=jnp.int32)
    which = stored // block_rows
    slots = jnp.arange(span_order.shape[1], dtype=jnp.int32)
    picked = jnp.sum(
        jnp.where(slots[None, None, :] == which[None, :, None], span_order[:, None, :], 0), axis=2
    )
    return picked * block_rows + stored % block_rows


def apply_rotation(value_rows, token_position, head_size):
    half = head_size // 2
    freqs = jnp.exp(-(2.0 * jnp.arange(half, dtype=jnp.float32) / head_size) * math.log(theta_base))
    angle = token_position.astype(jnp.float32)[..., None] * freqs
    cosine = jnp.cos(angle)[:, :, None, :]
    sine = jnp.sin(angle)[:, :, None, :]
    front = value_rows[..., :half]
    back = value_rows[..., half:]
    return jnp.concatenate([front * cosine - back * sine, back * cosine + front * sine], axis=-1)


def per_device(tokens, norm_gain, span_order, w_query, w_key, value_weight, w_out):
    sequence_batch, rows_dev, _ = tokens.shape
    head_size = HEAD_DIM
    query_heads = w_query.shape[1] // head_size
    key_heads = w_key.shape[1] // head_size
    group_width = query_heads // key_heads
    block_rows = rows_dev // 2
    total_rows = sequence_batch * rows_dev
    factor = 1.0 / math.sqrt(head_size)
    rank = lax.axis_index("ctx")
    whole = lax.all_gather(tokens, "tp", axis=2, tiled=True)
    normed = normalize(whole.reshape(total_rows, whole.shape[2]), norm_gain)
    query_pos = positions_of(span_order, rank * rows_dev, rows_dev, block_rows)
    latest = jnp.max(query_pos, axis=1)
    stat_shape = (sequence_batch, key_heads, group_width, rows_dev)
    initial = (
        jnp.full(stat_shape, masked_score, jnp.float32),
        jnp.zeros(stat_shape, jnp.float32),
        jnp.zeros(stat_shape + (head_size,), jnp.float32),
    )
    pieces = (
        lax.all_gather(w_query, "ctx", axis=0, tiled=True),
        lax.all_gather(w_key, "ctx", axis=0, tiled=True),
        lax.all_gather(value_weight, "ctx", axis=0, tiled=True),
    )
    query_flat, flattened_key, flattened_value = tuple(
        (jnp.dot(normed, piece, preferred_element_type=jnp.float32) for piece in pieces)
    )
    turned = apply_rotation(
        query_flat.reshape(sequence_batch, rows_dev, query_heads, head_size), query_pos, head_size
    ).astype(jnp.bfloat16)
    query = turned.reshape(sequence_batch, rows_dev, key_heads, group_width, head_size).transpose(
        0, 2, 3, 1, 4
    )
    turned = apply_rotation(
        flattened_key.reshape(sequence_batch, rows_dev, key_heads, head_size), query_pos, head_size
    ).astype(jnp.bfloat16)
    own_values = flattened_value.reshape(sequence_batch, rows_dev, key_heads, head_size).astype(
        jnp.bfloat16
    )
    key_piece = lax.all_gather(turned, "ctx", axis=1, tiled=True)
    value_piece = lax.all_gather(own_values, "ctx", axis=1, tiled=True)
    count = key_piece.shape[1]
    step_rows = 512

    def one_block(index, state):
        first = index * step_rows
        key_block = lax.dynamic_slice_in_dim(key_piece, first, step_rows, 1)
        value_block = lax.dynamic_slice_in_dim(value_piece, first, step_rows, 1)
        key_pos = positions_of(span_order, first, step_rows, block_rows)

        def update(current):
            peak, total, summed = current
            scores = (
                jnp.einsum(
                    "shgqd,skhd->shgqk", query, key_block, preferred_element_type=jnp.float32
                )
                * factor
            )
            allowed = key_pos[:, None, None, None, :] <= query_pos[:, None, None, :, None]
            scores = jnp.where(allowed, scores, masked_score)
            new_peak = jnp.maximum(peak, jnp.max(scores, axis=-1))
            weights = jnp.where(allowed, jnp.exp(scores - new_peak[..., None]), 0.0)
            shrink = jnp.exp(peak - new_peak)
            total = total * shrink + jnp.sum(weights, axis=-1)
            summed = summed * shrink[..., None] + jnp.einsum(
                "shgqk,skhd->shgqd",
                weights.astype(jnp.bfloat16),
                value_block,
                preferred_element_type=jnp.float32,
            )
            return (new_peak, total, summed)

        return lax.cond(
            jnp.all(jnp.min(key_pos, axis=1) > latest), lambda kept: kept, update, state
        )

    peak, total, summed = lax.fori_loop(0, count // step_rows, one_block, initial)
    attended = (summed / total[..., None]).astype(jnp.bfloat16)
    attended = attended.transpose(0, 3, 1, 2, 4).reshape(total_rows, query_heads * head_size)
    terms = jnp.dot(
        attended,
        lax.all_gather(w_out, "ctx", axis=1, tiled=True),
        preferred_element_type=jnp.float32,
    )
    mixed = lax.psum_scatter(terms.astype(jnp.bfloat16), "tp", scatter_dimension=1, tiled=True)
    return mixed.reshape(sequence_batch, rows_dev, mixed.shape[1])


def solution(mesh):
    placed = (
        P(None, "ctx", "tp"),
        P(),
        P(),
        P("ctx", "tp"),
        P("ctx", "tp"),
        P("ctx", "tp"),
        P("tp", "ctx"),
    )
    return jax.shard_map(
        per_device, mesh=mesh, in_specs=placed, out_specs=P(None, "ctx", "tp"), check_vma=False
    )
```

profile of v0, /device:TPU:0, one launch (start us, length us, event | category | flops | bytes accessed | tf_op | source)
XLA Modules:
  0.0 862.1 jit_solution(7252307660646929625)
XLA Ops:
  10.5 48.0 %all-gather.10.cloned.1.call-done = bf16[8192,256]{1,0:T(8,128)(2,1)} async-done(((bf16[1024,256]{1,0:T(8,128)(2,1)}), bf16[8192,256]{1,0:T(8,128)(2,1)}) %all-gather.10.cloned.1.call-update) | async-done | bytes 4194320 | tf_op jit(solution)/shard_map/all_gather | solution.py:62
  58.6 6.3 copy.24
  64.9 151.7 %all-gather.8.cloned.1.call-done = bf16[2,512,8192]{2,1,0:T(8,128)(2,1)} async-done(((bf16[2,512,2048]{2,1,0:T(8,128)(2,1)}), bf16[2,512,8192]{2,1,0:T(8,128)(2,1)}) %all-gather.8.cloned.1.call-update) | async-done | bytes 16777232 | tf_op jit(solution)/shard_map/all_gather | solution.py:50
  216.5 7.5 fusion.21
  224.0 9.0 %fusion.29 = f32[2,512,2,128]{1,3,2,0:T(8,128)S(1)} fusion(bf16[2,128,8192,1]{2,1,0,3:T(8,128)(2,1)S(1)} %bitcast.69, bf16[2,512,8192]{2,1,0:T(8,128)(2,1)} %all-gather.8.cloned.1.call-done, f32[8192]{0:T(1024)S(1)} %copy-done.2, f32[2,512]{1,0:T(2,128)S(1)} %add_rsqrt_fusion), kind=kOutput, calls=%fused_computation.49 | convolution fusion | flops 4328521728 | bytes 22056960 | tf_op jit(solution)/shard_map/dot_general | solution.py:66
  234.2 30.9 %all-gather.16.cloned.1.call-done = bf16[8192,256]{1,0:T(8,128)(2,1)} async-done(((bf16[1024,256]{1,0:T(8,128)(2,1)}), bf16[8192,256]{1,0:T(8,128)(2,1)}) %all-gather.16.cloned.1.call-update) | async-done | bytes 4194320 | tf_op jit(solution)/shard_map/all_gather | solution.py:63
  265.1 6.3 copy.28
  271.4 12.7 %convolution_convert_fusion.1 = bf16[2,512,2,128]{3,1,2,0:T(8,128)(2,1)} fusion(bf16[2,128,8192,1]{2,1,0,3:T(8,128)(2,1)} %bitcast.70, bf16[2,512,8192]{2,1,0:T(8,128)(2,1)} %all-gather.8.cloned.1.call-done, f32[8192]{0:T(1024)S(1)} %copy-done.2, f32[2,512]{1,0:T(2,128)S(1)} %add_rsqrt_fusion), kind=kOutput, calls=%fused_computation.47 | convolution fusion | flops 4328783872 | bytes 21532672 | tf_op jit(solution)/shard_map/dot_general | solution.py:66
  285.2 131.2 %all-gather.14.cloned.1.call-done = bf16[8192,1024]{1,0:T(8,128)(2,1)} async-done(((bf16[1024,1024]{1,0:T(8,128)(2,1)}), bf16[8192,1024]{1,0:T(8,128)(2,1)}) %all-gather.14.cloned.1.call-update) | async-done | bytes 16777232 | tf_op jit(solution)/shard_map/all_gather | solution.py:61
  416.4 21.4 %copy.25 = bf16[1024,8192]{1,0:T(8,128)(2,1)} copy(bf16[1024,8192]{0,1:T(8,128)(2,1)} %bitcast.63) | data formatting | bytes 33554432 | tf_op jit(solution)/shard_map/dot_general | solution.py:66
  437.9 22.4 %fusion.27 = f32[2,512,8,128]{1,3,2,0:T(8,128)S(1)} fusion(bf16[8,128,8192,1]{2,1,0,3:T(8,128)(2,1)} %bitcast.64, bf16[2,512,8192]{2,1,0:T(8,128)(2,1)} %all-gather.8.cloned.1.call-done, f32[8192]{0:T(1024)S(1)} %copy-done.2, f32[2,512]{1,0:T(2,128)S(1)} %add_rsqrt_fusion), kind=kOutput, calls=%fused_computation.48 | convolution fusion | flops 17213423616 | bytes 37785600 | tf_op jit(solution)/shard_map/dot_general | solution.py:66
  469.9 6.4 copy.29
  476.3 33.8 %all-gather.18.cloned.1.call-done = bf16[2,4096,2,128]{3,1,2,0:T(8,128)(2,1)} async-done(((bf16[2,512,2,128]{3,1,2,0:T(8,128)(2,1)}), bf16[2,4096,2,128]{3,1,2,0:T(8,128)(2,1)}) %all-gather.18.cloned.1.call-update) | async-done | bytes 4194320 | tf_op jit(solution)/shard_map/all_gather | solution.py:81
  512.6 156.1 %while.19 = (s32[]{:T(128)}, f32[2,2,4,512]{3,2,1,0:T(4,128)S(1)}, f32[2,2,4,512]{3,2,1,0:T(4,128)S(1)}, f32[2,2,4,512,128]{4,3,2,1,0:T(8,128)}, s32[2,16]{1,0:T...) while((s32[]{:T(128)}, f32[2,2,4,512]{3,2,1,0:T(4,128)S(1)}, ...), condition=%wide.region_11.12_spmd, body=%wide.region_3.11_spmd.sunk | while | flops 2204700672 | bytes 64532936 | solution.py:117
  514.2 17.9 %conditional.2 = (f32[2,2,4,512]{3,2,1,0:T(4,128)S(1)}, f32[2,2,4,512]{3,2,1,0:T(4,128)S(1)}, f32[2,2,4,512,128]{4,3,2,1,0:T(8,128)}) conditional(s32[]{:T(128)} %convert_element_type.85, (s32[2,512]{1,0:T(2,128)S(1)}, s32[2,512]{1,0:T(2,128)S(1)}, s32[]{:T(128)}, bf16[2,4096,2,128]{3,1,2,0:T(8,128)(2,1)}, bf16[2,2,4,512,128]{4,3,2,1,0:T(8,128)(2,1)}, ...), branch_computations={%region_7.9_spmd, %region_10.10_spmd} | conditional | flops 2204647424 | bytes 64430148 | solution.py:113
  514.6 4.7 fusion
  519.3 4.1 fusion.2
  523.5 8.7 %multiply_add_fusion = f32[2,2,4,512,128]{4,3,2,1,0:T(8,128)} fusion(f32[2,2,4,512,128]{4,3,2,1,0:T(8,128)} %get-tuple-element.360, f32[2,2,4,512]{3,2,1,0:T(4,128)S(1)} %bitcast.76, f32[2,2,512,4,512]{4,2,3,1,0:T(8,128)S(1)} %get-tuple-element.437, f32[2,2,4,512]{3,2,1,0:T(4,128)S(1)} %max.5, pred[2,512,512]{1,2,0:T(8,128)(4,1)S(1)} %broadcast_compare_fusion, ...), kind=kOutput, calls=%fused_computation.7 | convolution fusion | flops 1096810496 | bytes 26279940 | tf_op jit(solution)/shard_map/while/body/eval_jaxpr/cond/branch_0_fun/shgqk,skhd->shgqd/dot_general | solution.py:105
  533.8 17.9 %conditional.2 = (f32[2,2,4,512]{3,2,1,0:T(4,128)S(1)}, f32[2,2,4,512]{3,2,1,0:T(4,128)S(1)}, f32[2,2,4,512,128]{4,3,2,1,0:T(8,128)}) conditional(s32[]{:T(128)} %convert_element_type.85, (s32[2,512]{1,0:T(2,128)S(1)}, s32[2,512]{1,0:T(2,128)S(1)}, s32[]{:T(128)}, bf16[2,4096,2,128]{3,1,2,0:T(8,128)(2,1)}, bf16[2,2,4,512,128]{4,3,2,1,0:T(8,128)(2,1)}, ...), branch_computations={%region_7.9_spmd, %region_10.10_spmd} | conditional | flops 2204647424 | bytes 64430148 | solution.py:113
  534.2 4.7 fusion
  538.9 4.1 fusion.2
  543.0 8.7 %multiply_add_fusion = f32[2,2,4,512,128]{4,3,2,1,0:T(8,128)} fusion(f32[2,2,4,512,128]{4,3,2,1,0:T(8,128)} %get-tuple-element.360, f32[2,2,4,512]{3,2,1,0:T(4,128)S(1)} %bitcast.76, f32[2,2,512,4,512]{4,2,3,1,0:T(8,128)S(1)} %get-tuple-element.437, f32[2,2,4,512]{3,2,1,0:T(4,128)S(1)} %max.5, pred[2,512,512]{1,2,0:T(8,128)(4,1)S(1)} %broadcast_compare_fusion, ...), kind=kOutput, calls=%fused_computation.7 | convolution fusion | flops 1096810496 | bytes 26279940 | tf_op jit(solution)/shard_map/while/body/eval_jaxpr/cond/branch_0_fun/shgqk,skhd->shgqd/dot_general | solution.py:105
  553.3 17.9 %conditional.2 = (f32[2,2,4,512]{3,2,1,0:T(4,128)S(1)}, f32[2,2,4,512]{3,2,1,0:T(4,128)S(1)}, f32[2,2,4,512,128]{4,3,2,1,0:T(8,128)}) conditional(s32[]{:T(128)} %convert_element_type.85, (s32[2,512]{1,0:T(2,128)S(1)}, s32[2,512]{1,0:T(2,128)S(1)}, s32[]{:T(128)}, bf16[2,4096,2,128]{3,1,2,0:T(8,128)(2,1)}, bf16[2,2,4,512,128]{4,3,2,1,0:T(8,128)(2,1)}, ...), branch_computations={%region_7.9_spmd, %region_10.10_spmd} | conditional | flops 2204647424 | bytes 64430148 | solution.py:113
  553.7 4.7 fusion
  558.4 4.1 fusion.2
  562.5 8.7 %multiply_add_fusion = f32[2,2,4,512,128]{4,3,2,1,0:T(8,128)} fusion(f32[2,2,4,512,128]{4,3,2,1,0:T(8,128)} %get-tuple-element.360, f32[2,2,4,512]{3,2,1,0:T(4,128)S(1)} %bitcast.76, f32[2,2,512,4,512]{4,2,3,1,0:T(8,128)S(1)} %get-tuple-element.437, f32[2,2,4,512]{3,2,1,0:T(4,128)S(1)} %max.5, pred[2,512,512]{1,2,0:T(8,128)(4,1)S(1)} %broadcast_compare_fusion, ...), kind=kOutput, calls=%fused_computation.7 | convolution fusion | flops 1096810496 | bytes 26279940 | tf_op jit(solution)/shard_map/while/body/eval_jaxpr/cond/branch_0_fun/shgqk,skhd->shgqd/dot_general | solution.py:105
  572.8 17.9 %conditional.2 = (f32[2,2,4,512]{3,2,1,0:T(4,128)S(1)}, f32[2,2,4,512]{3,2,1,0:T(4,128)S(1)}, f32[2,2,4,512,128]{4,3,2,1,0:T(8,128)}) conditional(s32[]{:T(128)} %convert_element_type.85, (s32[2,512]{1,0:T(2,128)S(1)}, s32[2,512]{1,0:T(2,128)S(1)}, s32[]{:T(128)}, bf16[2,4096,2,128]{3,1,2,0:T(8,128)(2,1)}, bf16[2,2,4,512,128]{4,3,2,1,0:T(8,128)(2,1)}, ...), branch_computations={%region_7.9_spmd, %region_10.10_spmd} | conditional | flops 2204647424 | bytes 64430148 | solution.py:113
  573.2 4.7 fusion
  577.9 4.1 fusion.2
  582.0 8.7 %multiply_add_fusion = f32[2,2,4,512,128]{4,3,2,1,0:T(8,128)} fusion(f32[2,2,4,512,128]{4,3,2,1,0:T(8,128)} %get-tuple-element.360, f32[2,2,4,512]{3,2,1,0:T(4,128)S(1)} %bitcast.76, f32[2,2,512,4,512]{4,2,3,1,0:T(8,128)S(1)} %get-tuple-element.437, f32[2,2,4,512]{3,2,1,0:T(4,128)S(1)} %max.5, pred[2,512,512]{1,2,0:T(8,128)(4,1)S(1)} %broadcast_compare_fusion, ...), kind=kOutput, calls=%fused_computation.7 | convolution fusion | flops 1096810496 | bytes 26279940 | tf_op jit(solution)/shard_map/while/body/eval_jaxpr/cond/branch_0_fun/shgqk,skhd->shgqd/dot_general | solution.py:105
  592.3 17.9 %conditional.2 = (f32[2,2,4,512]{3,2,1,0:T(4,128)S(1)}, f32[2,2,4,512]{3,2,1,0:T(4,128)S(1)}, f32[2,2,4,512,128]{4,3,2,1,0:T(8,128)}) conditional(s32[]{:T(128)} %convert_element_type.85, (s32[2,512]{1,0:T(2,128)S(1)}, s32[2,512]{1,0:T(2,128)S(1)}, s32[]{:T(128)}, bf16[2,4096,2,128]{3,1,2,0:T(8,128)(2,1)}, bf16[2,2,4,512,128]{4,3,2,1,0:T(8,128)(2,1)}, ...), branch_computations={%region_7.9_spmd, %region_10.10_spmd} | conditional | flops 2204647424 | bytes 64430148 | solution.py:113
  592.7 4.8 fusion
  597.5 4.1 fusion.2
  601.7 8.6 multiply_add_fusion
  611.9 17.8 %conditional.2 = (f32[2,2,4,512]{3,2,1,0:T(4,128)S(1)}, f32[2,2,4,512]{3,2,1,0:T(4,128)S(1)}, f32[2,2,4,512,128]{4,3,2,1,0:T(8,128)}) conditional(s32[]{:T(128)} %convert_element_type.85, (s32[2,512]{1,0:T(2,128)S(1)}, s32[2,512]{1,0:T(2,128)S(1)}, s32[]{:T(128)}, bf16[2,4096,2,128]{3,1,2,0:T(8,128)(2,1)}, bf16[2,2,4,512,128]{4,3,2,1,0:T(8,128)(2,1)}, ...), branch_computations={%region_7.9_spmd, %region_10.10_spmd} | conditional | flops 2204647424 | bytes 64430148 | solution.py:113
  612.3 4.7 fusion
  617.0 4.1 fusion.2
  621.1 8.6 multiply_add_fusion
  631.4 17.8 %conditional.2 = (f32[2,2,4,512]{3,2,1,0:T(4,128)S(1)}, f32[2,2,4,512]{3,2,1,0:T(4,128)S(1)}, f32[2,2,4,512,128]{4,3,2,1,0:T(8,128)}) conditional(s32[]{:T(128)} %convert_element_type.85, (s32[2,512]{1,0:T(2,128)S(1)}, s32[2,512]{1,0:T(2,128)S(1)}, s32[]{:T(128)}, bf16[2,4096,2,128]{3,1,2,0:T(8,128)(2,1)}, bf16[2,2,4,512,128]{4,3,2,1,0:T(8,128)(2,1)}, ...), branch_computations={%region_7.9_spmd, %region_10.10_spmd} | conditional | flops 2204647424 | bytes 64430148 | solution.py:113
  631.7 4.7 fusion
  636.5 4.1 fusion.2
  640.6 8.6 multiply_add_fusion
  650.8 17.9 %conditional.2 = (f32[2,2,4,512]{3,2,1,0:T(4,128)S(1)}, f32[2,2,4,512]{3,2,1,0:T(4,128)S(1)}, f32[2,2,4,512,128]{4,3,2,1,0:T(8,128)}) conditional(s32[]{:T(128)} %convert_element_type.85, (s32[2,512]{1,0:T(2,128)S(1)}, s32[2,512]{1,0:T(2,128)S(1)}, s32[]{:T(128)}, bf16[2,4096,2,128]{3,1,2,0:T(8,128)(2,1)}, bf16[2,2,4,512,128]{4,3,2,1,0:T(8,128)(2,1)}, ...), branch_computations={%region_7.9_spmd, %region_10.10_spmd} | conditional | flops 2204647424 | bytes 64430148 | solution.py:113
  651.2 4.7 fusion
  655.9 4.1 fusion.2
  660.0 8.7 %multiply_add_fusion = f32[2,2,4,512,128]{4,3,2,1,0:T(8,128)} fusion(f32[2,2,4,512,128]{4,3,2,1,0:T(8,128)} %get-tuple-element.360, f32[2,2,4,512]{3,2,1,0:T(4,128)S(1)} %bitcast.76, f32[2,2,512,4,512]{4,2,3,1,0:T(8,128)S(1)} %get-tuple-element.437, f32[2,2,4,512]{3,2,1,0:T(4,128)S(1)} %max.5, pred[2,512,512]{1,2,0:T(8,128)(4,1)S(1)} %broadcast_compare_fusion, ...), kind=kOutput, calls=%fused_computation.7 | convolution fusion | flops 1096810496 | bytes 26279940 | tf_op jit(solution)/shard_map/while/body/eval_jaxpr/cond/branch_0_fun/shgqk,skhd->shgqd/dot_general | solution.py:105
  676.1 26.4 %convolution_convert_fusion = bf16[1024,8192]{1,0:T(8,128)(2,1)} fusion(bf16[1024,1024]{1,0:T(8,128)(2,1)} %reshape.213, bf16[1024,8192]{1,0:T(8,128)(2,1)} %all-gather.20.cloned.1.call-done), kind=kOutput, calls=%fused_computation.41 | convolution fusion | flops 17188257792 | bytes 35651584 | tf_op jit(solution)/shard_map/dot_general | solution.py:120
  702.6 152.7 %reduce-scatter.2.cloned.1.call-done = bf16[1024,2048]{1,0:T(8,128)(2,1)} async-done(((bf16[1024,8192]{1,0:T(8,128)(2,1)}), bf16[1024,2048]{1,0:T(8,128)(2,1)}) %reduce-scatter.2.cloned.1.call-update) | async-done | bytes 4194320 | tf_op jit(solution)/shard_map/reduce_scatter | solution.py:125
  (116 shorter events, 36.3 us)
Async XLA Ops:
  6.5 2.9 copy-start.1
  6.5 52.0 %all-gather.10.cloned.1.call-start = ((), (), s32[]{:S(2)}) async-start(), calls=%async_computation.2 | async-start | bytes 4718592 | tf_op jit(solution)/shard_map/all_gather | solution.py:62
  7.3 209.3 %all-gather.8.cloned.1.call-start = ((), (), s32[]{:S(2)}) async-start(), calls=%async_computation.1 | async-start | bytes 20971520 | tf_op jit(solution)/shard_map/all_gather | solution.py:50
  8.0 257.0 %all-gather.16.cloned.1.call-start = ((), (), s32[]{:S(2)}) async-start(), calls=%async_computation.5 | async-start | bytes 4718592 | tf_op jit(solution)/shard_map/all_gather | solution.py:63
  8.7 407.7 %all-gather.14.cloned.1.call-start = ((), (), s32[]{:S(2)}) async-start(), calls=%async_computation.4 | async-start | bytes 18874368 | tf_op jit(solution)/shard_map/all_gather | solution.py:61
  9.3 460.5 %all-gather.12.cloned.1.call-start = ((), (), s32[]{:S(2)}) async-start(), calls=%async_computation.3 | async-start | bytes 4718592 | tf_op jit(solution)/shard_map/all_gather | solution.py:80
  64.9 159.1 %copy-start.2 = (f32[8192]{0:T(1024)S(1)}, f32[8192]{0:T(1024)}, u32[]{:S(2)}) copy-start(f32[8192]{0:T(1024)} %param.12) | copy-start | bytes 98308
  216.5 7.5 copy-start
  234.1 276.0 %all-gather.18.cloned.1.call-start = ((), (), s32[]{:S(2)}) async-start(), calls=%async_computation.6 | async-start | bytes 4718592 | tf_op jit(solution)/shard_map/all_gather | solution.py:81
  284.1 392.1 %all-gather.20.cloned.1.call-start = ((), (), s32[]{:S(2)}) async-start(), calls=%async_computation.7 | async-start | bytes 18874368 | tf_op jit(solution)/shard_map/all_gather | solution.py:122
  284.8 570.4 %reduce-scatter.2.cloned.1.call-start = ((), (), s32[]{:S(2)}) async-start(), calls=%async_computation.8 | async-start | bytes 20971520 | tf_op jit(solution)/shard_map/reduce_scatter | solution.py:125
Sparse Core Ops, SparseCore 0:
  8.9 49.5 all-gather.9
  60.4 156.0 all-gather.7
  218.1 46.8 all-gather.15
  266.5 149.8 all-gather.13
  417.9 45.0 all-gather.11
  464.4 45.6 all-gather.17
  511.7 149.8 all-gather.19
  702.7 152.5 reduce-scatter.1
where the time goes:
time: 864 us; the launch traced here: 862 us
  waiting for transfers between devices  552 us (64%)
  matrix products  177 us (20%)
  other arithmetic  62 us (7%)
  local copies, waits for them, and re-layouts  51.1 us (6%)
  between operations  13.6 us (2%)
    reduce_scatter x1, waiting for transfers between devices, per_device(): lax.psum_scatter(terms.astype(jnp.bfloat16), 'tp', scatter_dimension=1, t...  153 us
    all_gather x1, waiting for transfers between devices, per_device(): whole = lax.all_gather(tokens, 'tp', axis=2, tiled=True)  152 us
    all_gather x1, waiting for transfers between devices, per_device(): lax.all_gather(w_query, 'ctx', axis=0, tiled=True)  131 us
    dot_general x8, matrix products, update(): jnp.einsum('shgqk,skhd->shgqd', weights.astype(jnp.bfloat16), value_block...  69.1 us
    all_gather x1, waiting for transfers between devices, per_device(): lax.all_gather(w_key, 'ctx', axis=0, tiled=True)  48 us
    dot_general x3, matrix products, per_device(): jnp.dot(normed, piece, preferred_element_type=jnp.float32)  44.1 us
    dot_general x8, matrix products, update(): jnp.einsum('shgqd,skhd->shgqk', query, key_block, preferred_element_type=...  37.6 us
    dot_general x3, local copies, waits for them, and re-layouts, per_device(): jnp.dot(normed, piece, preferred_element_type=jnp.float32)  34.1 us
  transfers between devices with their start and end apart: 8, of which 6 were waited for; matrix products, arithmetic and copies ran while one was open for 31% of the time, Pallas kernels for 0%

commit v1 on v0

--- a/solution.py
+++ b/solution.py
@@ -8,6 +8,18 @@
 theta_base = 500000.0
 norm_eps = 1e-05
 masked_score = -1e30
+
+
+def collect(value, axis, dim):
+    ways, here, step = (lax.axis_size(axis), lax.axis_index(axis), value.shape[dim])
+    line, have = (value, 1)
+    while have < ways:
+        line = jnp.concatenate(
+            [line, lax.ppermute(line, axis, [(d, (d - have) % ways) for d in range(ways)])],
+            axis=dim,
+        )
+        have = 2 * have
+    return jnp.roll(line, here * step, axis=dim)
 
 
 def normalize(flat_rows, norm_gain):
@@ -59,7 +71,7 @@
     )
     pieces = (
         lax.all_gather(w_query, "ctx", axis=0, tiled=True),
-        lax.all_gather(w_key, "ctx", axis=0, tiled=True),
+        collect(w_key, "ctx", 0),
         lax.all_gather(value_weight, "ctx", axis=0, tiled=True),
     )
     query_flat, flattened_key, flattened_value = tuple(

time: 864 us -> 817 us (0.946)
  waiting for transfers between devices: 552 us -> 491 us
    all_gather x1, waiting for transfers between devices: 152 us -> 19.1 us  [per_device(): whole = lax.all_gather(tokens, 'tp', axis=2, tiled=True)]
    ppermute x0 -> x3, waiting for transfers between devices: none -> 120 us  [collect(): lax.ppermute(line, axis, [(d, (d - have) % ways) for d in range(ways)])]
    all_gather x1 -> x0, waiting for transfers between devices: 48 us -> none  [per_device(): lax.all_gather(w_key, 'ctx', axis=0, tiled=True)]
    dot_general x3 -> x4, local copies, waits for them, and re-layouts: 34.1 us -> 36.4 us  [per_device(): jnp.dot(normed, piece, preferred_element_type=jnp.float32)]
  transfers between devices with their start and end apart: 8 -> 10, of which waited for: 6 -> 8; matrix products, arithmetic and copies ran while one was open for 31% -> 33% of each run, Pallas kernels for 0% -> 0%
where the time goes in v1:
time: 817 us; the launch traced here: 814 us
  waiting for transfers between devices  491 us (60%)
  matrix products  177 us (22%)
  other arithmetic  65.3 us (8%)
  local copies, waits for them, and re-layouts  56.2 us (7%)
  between operations  13.7 us (2%)
    reduce_scatter x1, waiting for transfers between devices, per_device(): lax.psum_scatter(terms.astype(jnp.bfloat16), 'tp', scatter_dimension=1, t...  153 us
    all_gather x1, waiting for transfers between devices, per_device(): lax.all_gather(w_query, 'ctx', axis=0, tiled=True)  132 us
    ppermute x3, waiting for transfers between devices, collect(): lax.ppermute(line, axis, [(d, (d - have) % ways) for d in range(ways)])  120 us
    dot_general x8, matrix products, update(): jnp.einsum('shgqk,skhd->shgqd', weights.astype(jnp.bfloat16), value_block...  69.1 us
    dot_general x3, matrix products, per_device(): jnp.dot(normed, piece, preferred_element_type=jnp.float32)  44.1 us
    dot_general x8, matrix products, update(): jnp.einsum('shgqd,skhd->shgqk', query, key_block, preferred_element_type=...  37.5 us
    dot_general x4, local copies, waits for them, and re-layouts, per_device(): jnp.dot(normed, piece, preferred_element_type=jnp.float32)  36.4 us
    all_gather x1, waiting for transfers between devices, per_device(): value_piece = lax.all_gather(own_values, 'ctx', axis=1, tiled=True)  33.8 us
  transfers between devices with their start and end apart: 10, of which 8 were waited for; matrix products, arithmetic and copies ran while one was open for 33% of the time, Pallas kernels for 0%

profile of v1, /device:TPU:0, one launch (start us, length us, event | category | flops | bytes accessed | tf_op | source)
XLA Modules:
  0.0 814.2 jit_solution(12348866576866406472)
XLA Ops:
  8.8 4.6 collective-permute-start
  13.4 7.0 collective-permute-done
  22.4 23.2 %collective-permute-done.1 = bf16[2048,256]{1,0:T(8,128)(2,1)S(1)} collective-permute-done((bf16[2048,256]{1,0:T(8,128)(2,1)S(1)}, bf16[2048,256]{1,0:T(8,128)(2,1)S(1)}, u32[]{:S(2)}, u32[]{:S(2)}) %collective-permute-start.1) | collective-permute-done | bytes 1048608 | tf_op jit(solution)/shard_map/ppermute | solution.py:18
  51.3 89.7 %collective-permute-done.2 = bf16[4096,256]{1,0:T(8,128)(2,1)S(1)} collective-permute-done((bf16[4096,256]{1,0:T(8,128)(2,1)}, bf16[4096,256]{1,0:T(8,128)(2,1)S(1)}, u32[]{:S(2)}, u32[]{:S(2)}) %collective-permute-start.2) | collective-permute-done | bytes 2097184 | tf_op jit(solution)/shard_map/ppermute | solution.py:18
  143.8 6.4 copy.24
  150.1 19.1 %all-gather.7.cloned.1.call-done = bf16[2,512,8192]{2,1,0:T(8,128)(2,1)} async-done(((bf16[2,512,2048]{2,1,0:T(8,128)(2,1)}), bf16[2,512,8192]{2,1,0:T(8,128)(2,1)}) %all-gather.7.cloned.1.call-update) | async-done | bytes 16777232 | tf_op jit(solution)/shard_map/all_gather | solution.py:62
  169.2 7.5 fusion.21
  176.7 9.0 %fusion.29 = f32[2,512,2,128]{1,3,2,0:T(8,128)S(1)} fusion(bf16[2,128,8192,1]{2,1,0,3:T(8,128)(2,1)S(1)} %bitcast.69, bf16[2,512,8192]{2,1,0:T(8,128)(2,1)} %all-gather.7.cloned.1.call-done, f32[8192]{0:T(1024)S(1)} %copy-done.7, f32[2,512]{1,0:T(2,128)S(1)} %add_rsqrt_fusion), kind=kOutput, calls=%fused_computation.52 | convolution fusion | flops 4328521728 | bytes 22056960 | tf_op jit(solution)/shard_map/dot_general | solution.py:78
  187.0 30.8 %all-gather.13.cloned.1.call-done = bf16[8192,256]{1,0:T(8,128)(2,1)} async-done(((bf16[1024,256]{1,0:T(8,128)(2,1)}), bf16[8192,256]{1,0:T(8,128)(2,1)}) %all-gather.13.cloned.1.call-update) | async-done | bytes 4194320 | tf_op jit(solution)/shard_map/all_gather | solution.py:75
  217.8 6.3 copy.28
  224.1 12.7 %convolution_convert_fusion.1 = bf16[2,512,2,128]{3,1,2,0:T(8,128)(2,1)} fusion(bf16[2,128,8192,1]{2,1,0,3:T(8,128)(2,1)} %bitcast.70, bf16[2,512,8192]{2,1,0:T(8,128)(2,1)} %all-gather.7.cloned.1.call-done, f32[8192]{0:T(1024)S(1)} %copy-done.7, f32[2,512]{1,0:T(2,128)S(1)} %add_rsqrt_fusion), kind=kOutput, calls=%fused_computation.49 | convolution fusion | flops 4328783872 | bytes 21532672 | tf_op jit(solution)/shard_map/dot_general | solution.py:78
  237.8 131.5 %all-gather.11.cloned.1.call-done = bf16[8192,1024]{1,0:T(8,128)(2,1)} async-done(((bf16[1024,1024]{1,0:T(8,128)(2,1)}), bf16[8192,1024]{1,0:T(8,128)(2,1)}) %all-gather.11.cloned.1.call-update) | async-done | bytes 16777232 | tf_op jit(solution)/shard_map/all_gather | solution.py:73
  369.3 21.5 %copy.25 = bf16[1024,8192]{1,0:T(8,128)(2,1)} copy(bf16[1024,8192]{0,1:T(8,128)(2,1)} %bitcast.64) | data formatting | bytes 33554432 | tf_op jit(solution)/shard_map/dot_general | solution.py:78
  390.8 22.4 %fusion.27 = f32[2,512,8,128]{1,3,2,0:T(8,128)S(1)} fusion(bf16[8,128,8192,1]{2,1,0,3:T(8,128)(2,1)} %bitcast.65, bf16[2,512,8192]{2,1,0:T(8,128)(2,1)} %all-gather.7.cloned.1.call-done, f32[8192]{0:T(1024)S(1)} %copy-done.7, f32[2,512]{1,0:T(2,128)S(1)} %add_rsqrt_fusion), kind=kOutput, calls=%fused_computation.51 | convolution fusion | flops 17213423616 | bytes 37785600 | tf_op jit(solution)/shard_map/dot_general | solution.py:78
  418.7 4.1 maximum_bitcast_fusion
  422.8 6.4 copy.29
  429.2 33.8 %all-gather.15.cloned.1.call-done = bf16[2,4096,2,128]{3,1,2,0:T(8,128)(2,1)} async-done(((bf16[2,512,2,128]{3,1,2,0:T(8,128)(2,1)}), bf16[2,4096,2,128]{3,1,2,0:T(8,128)(2,1)}) %all-gather.15.cloned.1.call-update) | async-done | bytes 4194320 | tf_op jit(solution)/shard_map/all_gather | solution.py:93
  465.4 155.1 %while.19 = (s32[]{:T(128)}, f32[2,2,4,512]{3,2,1,0:T(4,128)S(1)}, f32[2,2,4,512]{3,2,1,0:T(4,128)S(1)}, f32[2,2,4,512,128]{4,3,2,1,0:T(8,128)}, s32[2,16]{1,0:T...) while((s32[]{:T(128)}, f32[2,2,4,512]{3,2,1,0:T(4,128)S(1)}, ...), condition=%wide.region_11.12_spmd, body=%wide.region_3.11_spmd.sunk | while | flops 2204700672 | bytes 64532936 | solution.py:129
  467.0 17.9 %conditional.2 = (f32[2,2,4,512]{3,2,1,0:T(4,128)S(1)}, f32[2,2,4,512]{3,2,1,0:T(4,128)S(1)}, f32[2,2,4,512,128]{4,3,2,1,0:T(8,128)}) conditional(s32[]{:T(128)} %convert_element_type.85, (s32[2,512]{1,0:T(2,128)S(1)}, s32[2,512]{1,0:T(2,128)S(1)}, s32[]{:T(128)}, bf16[2,4096,2,128]{3,1,2,0:T(8,128)(2,1)}, bf16[2,2,4,512,128]{4,3,2,1,0:T(8,128)(2,1)}, ...), branch_computations={%region_7.9_spmd, %region_10.10_spmd} | conditional | flops 2204647424 | bytes 64430148 | solution.py:125
  467.4 4.7 fusion
  472.1 4.1 fusion.2
  476.2 8.7 %multiply_add_fusion = f32[2,2,4,512,128]{4,3,2,1,0:T(8,128)} fusion(f32[2,2,4,512,128]{4,3,2,1,0:T(8,128)} %get-tuple-element.360, f32[2,2,4,512]{3,2,1,0:T(4,128)S(1)} %bitcast.76, f32[2,2,512,4,512]{4,2,3,1,0:T(8,128)S(1)} %get-tuple-element.437, f32[2,2,4,512]{3,2,1,0:T(4,128)S(1)} %max.5, pred[2,512,512]{1,2,0:T(8,128)(4,1)S(1)} %broadcast_compare_fusion, ...), kind=kOutput, calls=%fused_computation.7 | convolution fusion | flops 1096810496 | bytes 26279940 | tf_op jit(solution)/shard_map/while/body/eval_jaxpr/cond/branch_0_fun/shgqk,skhd->shgqd/dot_general | solution.py:117
  486.4 17.9 %conditional.2 = (f32[2,2,4,512]{3,2,1,0:T(4,128)S(1)}, f32[2,2,4,512]{3,2,1,0:T(4,128)S(1)}, f32[2,2,4,512,128]{4,3,2,1,0:T(8,128)}) conditional(s32[]{:T(128)} %convert_element_type.85, (s32[2,512]{1,0:T(2,128)S(1)}, s32[2,512]{1,0:T(2,128)S(1)}, s32[]{:T(128)}, bf16[2,4096,2,128]{3,1,2,0:T(8,128)(2,1)}, bf16[2,2,4,512,128]{4,3,2,1,0:T(8,128)(2,1)}, ...), branch_computations={%region_7.9_spmd, %region_10.10_spmd} | conditional | flops 2204647424 | bytes 64430148 | solution.py:125
  486.8 4.7 fusion
  491.5 4.1 fusion.2
  495.6 8.7 %multiply_add_fusion = f32[2,2,4,512,128]{4,3,2,1,0:T(8,128)} fusion(f32[2,2,4,512,128]{4,3,2,1,0:T(8,128)} %get-tuple-element.360, f32[2,2,4,512]{3,2,1,0:T(4,128)S(1)} %bitcast.76, f32[2,2,512,4,512]{4,2,3,1,0:T(8,128)S(1)} %get-tuple-element.437, f32[2,2,4,512]{3,2,1,0:T(4,128)S(1)} %max.5, pred[2,512,512]{1,2,0:T(8,128)(4,1)S(1)} %broadcast_compare_fusion, ...), kind=kOutput, calls=%fused_computation.7 | convolution fusion | flops 1096810496 | bytes 26279940 | tf_op jit(solution)/shard_map/while/body/eval_jaxpr/cond/branch_0_fun/shgqk,skhd->shgqd/dot_general | solution.py:117
  505.8 17.8 %conditional.2 = (f32[2,2,4,512]{3,2,1,0:T(4,128)S(1)}, f32[2,2,4,512]{3,2,1,0:T(4,128)S(1)}, f32[2,2,4,512,128]{4,3,2,1,0:T(8,128)}) conditional(s32[]{:T(128)} %convert_element_type.85, (s32[2,512]{1,0:T(2,128)S(1)}, s32[2,512]{1,0:T(2,128)S(1)}, s32[]{:T(128)}, bf16[2,4096,2,128]{3,1,2,0:T(8,128)(2,1)}, bf16[2,2,4,512,128]{4,3,2,1,0:T(8,128)(2,1)}, ...), branch_computations={%region_7.9_spmd, %region_10.10_spmd} | conditional | flops 2204647424 | bytes 64430148 | solution.py:125
  506.2 4.7 fusion
  510.9 4.1 fusion.2
  515.0 8.6 %multiply_add_fusion = f32[2,2,4,512,128]{4,3,2,1,0:T(8,128)} fusion(f32[2,2,4,512,128]{4,3,2,1,0:T(8,128)} %get-tuple-element.360, f32[2,2,4,512]{3,2,1,0:T(4,128)S(1)} %bitcast.76, f32[2,2,512,4,512]{4,2,3,1,0:T(8,128)S(1)} %get-tuple-element.437, f32[2,2,4,512]{3,2,1,0:T(4,128)S(1)} %max.5, pred[2,512,512]{1,2,0:T(8,128)(4,1)S(1)} %broadcast_compare_fusion, ...), kind=kOutput, calls=%fused_computation.7 | convolution fusion | flops 1096810496 | bytes 26279940 | tf_op jit(solution)/shard_map/while/body/eval_jaxpr/cond/branch_0_fun/shgqk,skhd->shgqd/dot_general | solution.py:117
  525.2 18.0 %conditional.2 = (f32[2,2,4,512]{3,2,1,0:T(4,128)S(1)}, f32[2,2,4,512]{3,2,1,0:T(4,128)S(1)}, f32[2,2,4,512,128]{4,3,2,1,0:T(8,128)}) conditional(s32[]{:T(128)} %convert_element_type.85, (s32[2,512]{1,0:T(2,128)S(1)}, s32[2,512]{1,0:T(2,128)S(1)}, s32[]{:T(128)}, bf16[2,4096,2,128]{3,1,2,0:T(8,128)(2,1)}, bf16[2,2,4,512,128]{4,3,2,1,0:T(8,128)(2,1)}, ...), branch_computations={%region_7.9_spmd, %region_10.10_spmd} | conditional | flops 2204647424 | bytes 64430148 | solution.py:125
  525.6 4.7 fusion
  530.3 4.1 fusion.2
  534.4 8.7 %multiply_add_fusion = f32[2,2,4,512,128]{4,3,2,1,0:T(8,128)} fusion(f32[2,2,4,512,128]{4,3,2,1,0:T(8,128)} %get-tuple-element.360, f32[2,2,4,512]{3,2,1,0:T(4,128)S(1)} %bitcast.76, f32[2,2,512,4,512]{4,2,3,1,0:T(8,128)S(1)} %get-tuple-element.437, f32[2,2,4,512]{3,2,1,0:T(4,128)S(1)} %max.5, pred[2,512,512]{1,2,0:T(8,128)(4,1)S(1)} %broadcast_compare_fusion, ...), kind=kOutput, calls=%fused_computation.7 | convolution fusion | flops 1096810496 | bytes 26279940 | tf_op jit(solution)/shard_map/while/body/eval_jaxpr/cond/branch_0_fun/shgqk,skhd->shgqd/dot_general | solution.py:117
  544.6 17.8 %conditional.2 = (f32[2,2,4,512]{3,2,1,0:T(4,128)S(1)}, f32[2,2,4,512]{3,2,1,0:T(4,128)S(1)}, f32[2,2,4,512,128]{4,3,2,1,0:T(8,128)}) conditional(s32[]{:T(128)} %convert_element_type.85, (s32[2,512]{1,0:T(2,128)S(1)}, s32[2,512]{1,0:T(2,128)S(1)}, s32[]{:T(128)}, bf16[2,4096,2,128]{3,1,2,0:T(8,128)(2,1)}, bf16[2,2,4,512,128]{4,3,2,1,0:T(8,128)(2,1)}, ...), branch_computations={%region_7.9_spmd, %region_10.10_spmd} | conditional | flops 2204647424 | bytes 64430148 | solution.py:125
  545.0 4.7 fusion
  553.9 8.6 %multiply_add_fusion = f32[2,2,4,512,128]{4,3,2,1,0:T(8,128)} fusion(f32[2,2,4,512,128]{4,3,2,1,0:T(8,128)} %get-tuple-element.360, f32[2,2,4,512]{3,2,1,0:T(4,128)S(1)} %bitcast.76, f32[2,2,512,4,512]{4,2,3,1,0:T(8,128)S(1)} %get-tuple-element.437, f32[2,2,4,512]{3,2,1,0:T(4,128)S(1)} %max.5, pred[2,512,512]{1,2,0:T(8,128)(4,1)S(1)} %broadcast_compare_fusion, ...), kind=kOutput, calls=%fused_computation.7 | convolution fusion | flops 1096810496 | bytes 26279940 | tf_op jit(solution)/shard_map/while/body/eval_jaxpr/cond/branch_0_fun/shgqk,skhd->shgqd/dot_general | solution.py:117
  564.0 17.8 %conditional.2 = (f32[2,2,4,512]{3,2,1,0:T(4,128)S(1)}, f32[2,2,4,512]{3,2,1,0:T(4,128)S(1)}, f32[2,2,4,512,128]{4,3,2,1,0:T(8,128)}) conditional(s32[]{:T(128)} %convert_element_type.85, (s32[2,512]{1,0:T(2,128)S(1)}, s32[2,512]{1,0:T(2,128)S(1)}, s32[]{:T(128)}, bf16[2,4096,2,128]{3,1,2,0:T(8,128)(2,1)}, bf16[2,2,4,512,128]{4,3,2,1,0:T(8,128)(2,1)}, ...), branch_computations={%region_7.9_spmd, %region_10.10_spmd} | conditional | flops 2204647424 | bytes 64430148 | solution.py:125
  564.4 4.7 fusion
  573.2 8.6 %multiply_add_fusion = f32[2,2,4,512,128]{4,3,2,1,0:T(8,128)} fusion(f32[2,2,4,512,128]{4,3,2,1,0:T(8,128)} %get-tuple-element.360, f32[2,2,4,512]{3,2,1,0:T(4,128)S(1)} %bitcast.76, f32[2,2,512,4,512]{4,2,3,1,0:T(8,128)S(1)} %get-tuple-element.437, f32[2,2,4,512]{3,2,1,0:T(4,128)S(1)} %max.5, pred[2,512,512]{1,2,0:T(8,128)(4,1)S(1)} %broadcast_compare_fusion, ...), kind=kOutput, calls=%fused_computation.7 | convolution fusion | flops 1096810496 | bytes 26279940 | tf_op jit(solution)/shard_map/while/body/eval_jaxpr/cond/branch_0_fun/shgqk,skhd->shgqd/dot_general | solution.py:117
  583.3 17.8 %conditional.2 = (f32[2,2,4,512]{3,2,1,0:T(4,128)S(1)}, f32[2,2,4,512]{3,2,1,0:T(4,128)S(1)}, f32[2,2,4,512,128]{4,3,2,1,0:T(8,128)}) conditional(s32[]{:T(128)} %convert_element_type.85, (s32[2,512]{1,0:T(2,128)S(1)}, s32[2,512]{1,0:T(2,128)S(1)}, s32[]{:T(128)}, bf16[2,4096,2,128]{3,1,2,0:T(8,128)(2,1)}, bf16[2,2,4,512,128]{4,3,2,1,0:T(8,128)(2,1)}, ...), branch_computations={%region_7.9_spmd, %region_10.10_spmd} | conditional | flops 2204647424 | bytes 64430148 | solution.py:125
  583.7 4.7 fusion
  592.6 8.6 %multiply_add_fusion = f32[2,2,4,512,128]{4,3,2,1,0:T(8,128)} fusion(f32[2,2,4,512,128]{4,3,2,1,0:T(8,128)} %get-tuple-element.360, f32[2,2,4,512]{3,2,1,0:T(4,128)S(1)} %bitcast.76, f32[2,2,512,4,512]{4,2,3,1,0:T(8,128)S(1)} %get-tuple-element.437, f32[2,2,4,512]{3,2,1,0:T(4,128)S(1)} %max.5, pred[2,512,512]{1,2,0:T(8,128)(4,1)S(1)} %broadcast_compare_fusion, ...), kind=kOutput, calls=%fused_computation.7 | convolution fusion | flops 1096810496 | bytes 26279940 | tf_op jit(solution)/shard_map/while/body/eval_jaxpr/cond/branch_0_fun/shgqk,skhd->shgqd/dot_general | solution.py:117
  602.7 17.8 %conditional.2 = (f32[2,2,4,512]{3,2,1,0:T(4,128)S(1)}, f32[2,2,4,512]{3,2,1,0:T(4,128)S(1)}, f32[2,2,4,512,128]{4,3,2,1,0:T(8,128)}) conditional(s32[]{:T(128)} %convert_element_type.85, (s32[2,512]{1,0:T(2,128)S(1)}, s32[2,512]{1,0:T(2,128)S(1)}, s32[]{:T(128)}, bf16[2,4096,2,128]{3,1,2,0:T(8,128)(2,1)}, bf16[2,2,4,512,128]{4,3,2,1,0:T(8,128)(2,1)}, ...), branch_computations={%region_7.9_spmd, %region_10.10_spmd} | conditional | flops 2204647424 | bytes 64430148 | solution.py:125
  603.1 4.7 fusion
  611.9 8.6 %multiply_add_fusion = f32[2,2,4,512,128]{4,3,2,1,0:T(8,128)} fusion(f32[2,2,4,512,128]{4,3,2,1,0:T(8,128)} %get-tuple-element.360, f32[2,2,4,512]{3,2,1,0:T(4,128)S(1)} %bitcast.76, f32[2,2,512,4,512]{4,2,3,1,0:T(8,128)S(1)} %get-tuple-element.437, f32[2,2,4,512]{3,2,1,0:T(4,128)S(1)} %max.5, pred[2,512,512]{1,2,0:T(8,128)(4,1)S(1)} %broadcast_compare_fusion, ...), kind=kOutput, calls=%fused_computation.7 | convolution fusion | flops 1096810496 | bytes 26279940 | tf_op jit(solution)/shard_map/while/body/eval_jaxpr/cond/branch_0_fun/shgqk,skhd->shgqd/dot_general | solution.py:117
  627.9 26.4 %convolution_convert_fusion = bf16[1024,8192]{1,0:T(8,128)(2,1)} fusion(bf16[1024,1024]{1,0:T(8,128)(2,1)} %reshape.213, bf16[1024,8192]{1,0:T(8,128)(2,1)} %all-gather.17.cloned.1.call-done), kind=kOutput, calls=%fused_computation.41 | convolution fusion | flops 17188257792 | bytes 35651584 | tf_op jit(solution)/shard_map/dot_general | solution.py:132
  654.4 153.0 %reduce-scatter.2.cloned.1.call-done = bf16[1024,2048]{1,0:T(8,128)(2,1)} async-done(((bf16[1024,8192]{1,0:T(8,128)(2,1)}), bf16[1024,2048]{1,0:T(8,128)(2,1)}) %reduce-scatter.2.cloned.1.call-update) | async-done | bytes 4194320 | tf_op jit(solution)/shard_map/reduce_scatter | solution.py:137
  (140 shorter events, 56.6 us)
Async XLA Ops:
  6.5 39.1 %copy-start = (bf16[1024,256]{1,0:T(8,128)(2,1)S(1)}, bf16[1024,256]{1,0:T(8,128)(2,1)}, u32[]{:S(2)}) copy-start(bf16[1024,256]{1,0:T(8,128)(2,1)} %param.15) | copy-start | bytes 1572868
  6.5 40.6 %copy-start.6 = (s32[2,16]{1,0:T(2,128)S(1)}, s32[2,16]{1,0:T(2,128)}, u32[]{:S(2)}) copy-start(s32[2,16]{1,0:T(2,128)} %param.13) | copy-start | bytes 388
  6.5 162.7 %all-gather.7.cloned.1.call-start = ((), (), s32[]{:S(2)}) async-start(), calls=%async_computation.1 | async-start | bytes 20971520 | tf_op jit(solution)/shard_map/all_gather | solution.py:62
  7.3 210.5 %all-gather.13.cloned.1.call-start = ((), (), s32[]{:S(2)}) async-start(), calls=%async_computation.4 | async-start | bytes 4718592 | tf_op jit(solution)/shard_map/all_gather | solution.py:75
  8.0 361.3 %all-gather.11.cloned.1.call-start = ((), (), s32[]{:S(2)}) async-start(), calls=%async_computation.3 | async-start | bytes 18874368 | tf_op jit(solution)/shard_map/all_gather | solution.py:73
  8.7 414.0 %all-gather.9.cloned.1.call-start = ((), (), s32[]{:S(2)}) async-start(), calls=%async_computation.2 | async-start | bytes 4718592 | tf_op jit(solution)/shard_map/all_gather | solution.py:92
  8.8 11.6 %collective-permute-start = (bf16[1024,256]{1,0:T(8,128)(2,1)}, bf16[1024,256]{1,0:T(8,128)(2,1)S(1)}, u32[]{:S(2)}, u32[]{:S(2)}) collective-permute-start(bf16[1024,256]{1,0:T(8,128)(2,1)} %param.15), channel_id=1, source_target_pairs={{0,28},{4,0},{8,4},{12,8},{16,12},{20,16},{24,20},{28,24},{1,29},{... | collective-permute-start | bytes 1572872 | tf_op jit(solution)/shard_map/ppermute | solution.py:18
  20.4 26.7 %copy-start.2 = (bf16[1024,256]{1,0:T(8,128)(2,1)}, bf16[1024,256]{1,0:T(8,128)(2,1)S(1)}, u32[]{:S(2)}) copy-start(bf16[1024,256]{1,0:T(8,128)(2,1)S(1)} %collective-permute-done) | copy-start | bytes 1572868
  21.8 23.7 %collective-permute-start.1 = (bf16[2048,256]{1,0:T(8,128)(2,1)S(1)}, bf16[2048,256]{1,0:T(8,128)(2,1)S(1)}, u32[]{:S(2)}, u32[]{:S(2)}) collective-permute-start(bf16[2048,256]{1,0:T(8,128)(2,1)S(1)} %pad_maximum_fusion.1), channel_id=1, source_target_pairs={{0,24},{4,28},{8,0},{12,4},{16,8},{20,12},{24,16},{28,20},{1,25},{... | collective-permute-start | bytes 3145736 | tf_op jit(solution)/shard_map/ppermute | solution.py:18
  47.1 94.0 %collective-permute-start.2 = (bf16[4096,256]{1,0:T(8,128)(2,1)}, bf16[4096,256]{1,0:T(8,128)(2,1)S(1)}, u32[]{:S(2)}, u32[]{:S(2)}) collective-permute-start(bf16[4096,256]{1,0:T(8,128)(2,1)} %pad_maximum_fusion), channel_id=1, source_target_pairs={{0,16},{4,20},{8,24},{12,28},{16,0},{20,4},{24,8},{28,12},{1,17},{... | collective-permute-start | bytes 6291464 | tf_op jit(solution)/shard_map/ppermute | solution.py:18
  47.1 94.1 %copy-start.1 = (bf16[1024,256]{1,0:T(8,128)(2,1)S(1)}, bf16[1024,256]{1,0:T(8,128)(2,1)}, u32[]{:S(2)}) copy-start(bf16[1024,256]{1,0:T(8,128)(2,1)} %param.15) | copy-start | bytes 1572868
  47.1 94.1 %copy-start.3 = (bf16[1024,256]{1,0:T(8,128)(2,1)S(1)}, bf16[1024,256]{1,0:T(8,128)(2,1)}, u32[]{:S(2)}) copy-start(bf16[1024,256]{1,0:T(8,128)(2,1)} %copy-done.2) | copy-start | bytes 1572868
  150.1 26.6 %copy-start.7 = (f32[8192]{0:T(1024)S(1)}, f32[8192]{0:T(1024)}, u32[]{:S(2)}) copy-start(f32[8192]{0:T(1024)} %param.12) | copy-start | bytes 98308
  169.2 7.5 copy-start.4
  176.7 9.1 %copy-start.5 = (f32[2,512,64]{1,2,0:T(8,128)S(1)}, f32[2,512,64]{1,2,0:T(8,128)}, u32[]{:S(2)}) copy-start(f32[2,512,64]{1,2,0:T(8,128)} %get-tuple-element.445) | copy-start | bytes 786436
  186.9 276.1 %all-gather.15.cloned.1.call-start = ((), (), s32[]{:S(2)}) async-start(), calls=%async_computation.5 | async-start | bytes 4718592 | tf_op jit(solution)/shard_map/all_gather | solution.py:93
  236.8 391.1 %all-gather.17.cloned.1.call-start = ((), (), s32[]{:S(2)}) async-start(), calls=%async_computation.6 | async-start | bytes 18874368 | tf_op jit(solution)/shard_map/all_gather | solution.py:134
  237.4 569.9 %reduce-scatter.2.cloned.1.call-start = ((), (), s32[]{:S(2)}) async-start(), calls=%async_computation.7 | async-start | bytes 20971520 | tf_op jit(solution)/shard_map/reduce_scatter | solution.py:137
Sparse Core Ops, SparseCore 0:
  9.2 160.0 all-gather.6
  170.8 46.8 all-gather.12
  219.4 149.8 all-gather.10
  370.7 45.0 all-gather.8
  417.3 45.6 all-gather.14
  464.4 149.8 all-gather.16
  654.5 152.8 reduce-scatter.1
